TPU v7x, 128 devices: a whole 4x4x4 slice. The times are simulated.
128 devices in a mesh: tm: 128 (over x, z, y, core).
Axes of the slice: x: 4, y: 4, z: 4, core: 2. Of those that a mesh axis runs over, the one named last changes fastest.
Arguments:
- field: bfloat16 [43008, 8192], P('tm'), may hold values from -52 to 52
- index: float32 [43008, 10], P('tm'), may hold values from -13 to 13
- lag_list: int32 [61], replicated, may hold values from -30 to 30, as said below
- index_offset: int32 [10], replicated, may hold values from 0 to 14, as said below
- sea_mask: int32 [8192], P('tm'), may hold values 0 or 1
Outputs:
- corr_maps: float32 [8192, 10, 61], P('tm')
Inputs may be any that keep to these rules, and one draw needn't show every extreme that they name: `lag_list`: each whole number of -30 to 30 appears once. `index_offset`: some index has the extra lead 14.
All inputs are finite; a program needn't handle non-finite values. No bound on the sum of `sea_mask` on one device may be relied on, other than what follows from the above.
Results may differ from a plain program's by a relative error of at most 0.00051.
Values may be sent and summed in bfloat16 or wider, within the bound.
A program may use at most 256 MiB of HBM per device.

v0:
```python
import jax
import jax.numpy as jnp
from jax import lax
from jax.experimental import pallas as pl
from jax.experimental.pallas import tpu as pltpu
from jax.sharding import Mesh
from jax.sharding import PartitionSpec as P

MAXLAG = 30
MAXOFF = 14
LAGS = 61
KC = 10
T_DEV = 336
N_CHIP = 64
CELLS = 8192
TDAYS = 43008
TM = ("x", "z", "y", "core")
MESH = pl.DeviceIdType.MESH

K = 2 * T_DEV
KP = 768
R = 208
PR = 204
G = R // 16
HG = 7
LC = 896
QMAX = 32000.0
FAR = 1e9
I32 = jnp.int32
F32 = jnp.float32
BF = jnp.bfloat16


def pieces():
    out = []
    for k in range(KC):
        r = k * LAGS
        end = r + LAGS
        while r < end:
            p = r // PR
            stop = min(end, (p + 1) * PR)
            out.append((k, r - k * LAGS, stop - r, p, r - p * PR))
            r = stop
    return out


def onehot3(t):
    return (2 - t) * (1 - t) // 2, t * (2 - t), t * (t - 1) // 2


def rows(g):
    return pl.ds(16 * g, 16)


def encode(chunk, put, width, raw=None):
    m = jnp.abs(chunk(0))
    for g in range(1, G):
        m = jnp.maximum(m, jnp.abs(chunk(g)))
    m = jnp.max(m, axis=0, keepdims=True)
    e = jnp.ceil(jnp.log2(jnp.maximum(m, 1e-30)))
    scale = QMAX * jnp.exp2(-e)
    last = lax.broadcasted_iota(I32, (16, width), 0) == 15
    for g in range(G):
        q = jnp.round(chunk(g) * scale)
        if g == G - 1:
            q = jnp.where(last, jnp.broadcast_to(e, (16, width)), q)
        if raw is not None:
            raw.append(q)
            continue
        q = q.astype(I32).astype(jnp.int16)
        for i in range(width // 128):
            put(g, i, q[:, 128 * i : 128 * (i + 1)])


def fold(chunks, h, lane):
    out = []
    for g in range(HG):
        lo = chunks[g]
        hi = chunks[g + HG] if g + HG < G else jnp.zeros((16, 128), F32)
        if h:
            out.append(jnp.where(lane < 64, pltpu.roll(lo, 64, axis=1), hi))
        else:
            out.append(jnp.where(lane < 64, lo, pltpu.roll(hi, 64, axis=1)))
    return out


def decode_folded(get):
    lane = lax.broadcasted_iota(I32, (16, 128), 1)
    row = lax.broadcasted_iota(I32, (16, 128), 0)
    out = [get(g).astype(I32).astype(F32) for g in range(HG)]
    e = out[G - 1 - HG][15:16, :]
    e = jnp.where(lane[0:1] < 64, pltpu.roll(jnp.broadcast_to(e, (8, 128)), 64, axis=1)[0:1], e)
    scale = jnp.exp2(e) * (1.0 / QMAX)
    out = [v * scale for v in out]
    out[G - 1 - HG] = jnp.where((row == 15) & (lane >= 64), 0.0, out[G - 1 - HG])
    return out


def decode(get):
    tail = get(G - 1).astype(I32).astype(F32)
    scale = jnp.exp2(tail[15:16, :]) * (1.0 / QMAX)
    last = lax.broadcasted_iota(I32, (16, 128), 0) == 15
    out = [get(g).astype(I32).astype(F32) * scale for g in range(G - 1)]
    out.append(jnp.where(last, 0.0, tail * scale))
    return out


def main_kernel(
    field, idx_in, offs_in, fin, sums_o, tot_o, stat_o,
    idx, offs, sem_in, F, W, WF, OH, acc, NP, S1,
    s_far, r_far, s_n, r_n, s2f, r2f, s2n, r2n, s3, r3,
    iw, ipad, bs, g1, g2, fsum, sx_s, sx_r, tb1, sy_r, tb2, sz_r, tb3,
    sem_loc, sem_fs, sem_fr, sem_is, sem_ir, sem_gs, sem_g1, sem_g2,
    sem_far, sem_n, sem_2f, sem_2n, sem_3,
    sem_sfar, sem_sn, sem_s2f, sem_s2n, sem_s3, sem_ss, sem_sr, sem_os, sem_or, sem_bs, sem_br,
):
    X, Z, Y, C = (lax.axis_index(a) for a in TM)
    Q = (X * 4 + Z) * 4 + Y

    def peer(dx=0, dz=0, dy=0, dc=0):
        return {
            "x": (X + dx) % 4,
            "z": (Z + dz) % 4,
            "y": (Y + dy) % 4,
            "core": (C + dc) % 2,
        }

    def chip_peer(q, core):
        return {"x": q // 16, "z": (q // 4) % 4, "y": q % 4, "core": core}

    def along(t, delta, dc=0):
        f0, f1, f2 = onehot3(t)
        return peer(dx=f0 * delta, dy=f1 * delta, dz=f2 * delta, dc=dc)

    partner = peer(dc=1)
    xpeers = [(dx, dc) for dx in range(4) for dc in range(2) if dx or dc]
    yzpeers = [(dy, dz) for dy in range(4) for dz in range(4) if dy or dz]
    q_next, q_prev = (Q + 1) % N_CHIP, (Q + N_CHIP - 1) % N_CHIP

    copies = [
        pltpu.make_async_copy(idx_in, idx, sem_in.at[0]),
        pltpu.make_async_copy(offs_in, offs, sem_in.at[1]),
    ]
    for c in copies:
        c.start()

    barrier = pltpu.get_barrier_semaphore()

    def greet(device):
        pl.semaphore_signal(barrier, inc=1, device_id=device, device_id_type=MESH)

    for dx, dc in xpeers:
        greet(peer(dx=dx, dc=dc))
    for dy, dz in yzpeers:
        greet(peer(dy=dy, dz=dz))
    for d in range(1, 4):
        greet(peer(dy=d, dc=1))
        greet(peer(dz=d, dc=1))
    for q in (q_next, q_prev):
        for core in range(2):
            greet(chip_peer(q, core))

    def tile_of(slot, core):
        jx, jz, h = slot // 8, (slot // 2) % 4, slot % 2
        jy = 2 * h + (core + jx + jz) % 2
        return (jx * 4 + jz) * 4 + jy

    def columns(slot, core):
        return pl.ds(pl.multiple_of(tile_of(slot, core) * 128, 128), 128)

    own_days = pl.ds(pl.multiple_of(C * T_DEV, 16), T_DEV)

    eye = lax.broadcasted_iota(I32, (16, 128), 0) == lax.broadcasted_iota(I32, (16, 128), 1)

    def as_row(col):
        return jnp.sum(jnp.where(eye[:KC], col, 0.0), axis=0, keepdims=True)

    for c in copies:
        c.wait()
    mine = idx[...]
    me8, me16 = X * 2 + C, Y * 4 + Z
    g1[me8, 0:1, :] = as_row(jnp.sum(mine, axis=1, keepdims=True))
    g1[me8, 1:2, :] = as_row(jnp.sum(mine * mine, axis=1, keepdims=True))

    pl.semaphore_wait(barrier, 32)

    def remote(src, dst, ssem, rsem, device):
        return pltpu.make_async_remote_copy(
            src_ref=src, dst_ref=dst, send_sem=ssem, recv_sem=rsem,
            device_id=device, device_id_type=MESH,
        )

    g1c = [
        remote(g1.at[me8], g1.at[me8], sem_gs.at[i], sem_g1.at[i], peer(dx=dx, dc=dc))
        for i, (dx, dc) in enumerate(xpeers)
    ]
    for c in g1c:
        c.start()
    beside = (Q + N_CHIP + 2 * C - 1) % N_CHIP
    iwc = [remote(idx, iw.at[2], sem_is.at[2], sem_ir.at[2], partner)]
    for core in range(2):
        iwc.append(
            remote(
                idx, iw.at[1 - C], sem_is.at[core], sem_ir.at[1 - C], chip_peer(beside, core)
            )
        )
    for c in iwc:
        c.start()

    def share(begin, end):
        @pl.loop(begin, end)
        def _(s):
            remote(
                field.at[:, columns(s, 1 - C)], F.at[s, own_days, :], sem_fs, sem_fr, partner
            ).start()

    @pl.loop(0, 32)
    def _(s):
        pltpu.make_async_copy(
            field.at[:, columns(s, C)], F.at[s, own_days, :], sem_loc
        ).start()

    share(0, 10)

    @pl.loop(0, 32)
    def _(s):
        F[s, K:KP, :] = jnp.zeros((KP - K, 128), BF)

    for i in range(4):
        ipad[i] = jnp.zeros((16, 384), F32)
    ipad[3, 0:KC, 0:T_DEV] = mine

    for c in g1c:
        c.wait_recv()
    g = ((g1[0] + g1[1]) + (g1[2] + g1[3])) + ((g1[4] + g1[5]) + (g1[6] + g1[7]))
    g2[me16] = g
    g2c = [
        remote(
            g2.at[me16], g2.at[me16], sem_gs.at[7 + i], sem_g2.at[i], peer(dy=dy, dz=dz)
        )
        for i, (dy, dz) in enumerate(yzpeers)
    ]
    for c in g2c:
        c.start()
    share(10, 32)

    def cell_sums(start, fresh):
        @pl.loop(0, 32)
        def _(s):
            one = two = jnp.zeros((16, 128), F32)
            for g in range(T_DEV // 16):
                v = F[s, pl.ds(pl.multiple_of(start + 16 * g, 16), 16), :].astype(F32)
                one, two = one + v, two + v * v
            one = jnp.sum(one, axis=0, keepdims=True)
            two = jnp.sum(two, axis=0, keepdims=True)
            if not fresh:
                one, two = one + fsum[s, 0:1, :], two + fsum[s, 1:2, :]
            fsum[s, 0:1, :] = one
            fsum[s, 1:2, :] = two

    pltpu.make_async_copy(F.at[:, own_days, :], F.at[:, own_days, :], sem_loc).wait()
    cell_sums(C * T_DEV, True)
    for i in range(3):
        pltpu.make_async_copy(iw.at[i], iw.at[i], sem_ir.at[i]).wait()
        ipad[i, 0:KC, 0:T_DEV] = iw[i]
    pos = lax.broadcasted_iota(I32, (16, LC), 1)

    def placed(piece, at):
        wide = jnp.concatenate([piece, jnp.zeros((16, LC - 384), F32)], axis=1)
        return pltpu.roll(wide, at % LC, axis=1)

    mine, other = ipad[3], ipad[2]
    fc = C.astype(F32)
    w0 = mine * (1.0 - fc) + other * fc
    w1 = mine * fc + other * (1.0 - fc)
    series = jnp.where(
        pos < 64,
        placed(ipad[0], 64 - T_DEV),
        jnp.where(
            pos < 64 + T_DEV,
            placed(w0, 64),
            jnp.where(pos < 64 + K, placed(w1, 64 + T_DEV), placed(ipad[1], 64 + K)),
        ),
    )
    day = Q * K - 64 + pos
    series = jnp.where((day >= 0) & (day < TDAYS), series, FAR)
    kth = lax.broadcasted_iota(I32, (16, LC), 0)
    off = jnp.zeros((16, LC), I32)
    for k in range(KC):
        off = jnp.where(kth == k, offs[k], off)
    shifted = series
    for o in range(1, MAXOFF + 1):
        shifted = jnp.where(off == o, pltpu.roll(series, o, axis=1), shifted)
    tail = lax.broadcasted_iota(I32, (LAGS, KP), 1) < K
    lane_r = lax.broadcasted_iota(I32, (R, 128), 1)
    for p in range(3):
        lo = PR if p < 2 else KC * LAGS - 2 * PR
        WF[p, lo - lo % 8 : R, :] = jnp.full((R - lo + lo % 8, KP), FAR, F32)
        r = lax.broadcasted_iota(I32, (R, 128), 0) + PR * p
        OH[p] = jnp.where((r >= lane_r * LAGS) & (r < lane_r * LAGS + LAGS), 1.0, 0.0)
    todo = pieces()
    for k in range(KC):
        x = jnp.broadcast_to(shifted[k : k + 1, :], (64, LC))
        x = pltpu.roll(x, LC - 64 - MAXLAG, axis=1, stride=1, stride_axis=0)
        x = jnp.where(tail, x[:LAGS, :KP], FAR)
        for kk, a, n, p, b in todo:
            if kk == k:
                WF[p, b : b + n, :] = x[a : a + n, :]

    for c in g2c:
        c.wait_recv()
    g = g2[0]
    for i in range(1, 16):
        g = g + g2[i]
    mean_row = g[0:1, :] / float(TDAYS)
    stat_o[...] = jnp.zeros((8, 128), F32)
    stat_o[0:1, :] = mean_row
    stat_o[1:2, :] = g[1:2, :] / float(TDAYS) - mean_row * mean_row

    def center(p):
        col = jnp.sum(OH[p] * mean_row, axis=1, keepdims=True)
        for g in range(G):
            x = WF[p, rows(g), :]
            x = jnp.where(x > 0.5 * FAR, 0.0, x - col[16 * g : 16 * g + 16])
            W[p, rows(g), :] = x.astype(BF)

    pltpu.make_async_copy(F.at[:, own_days, :], F.at[:, own_days, :], sem_fr).wait()

    def part_coords(p):
        e0, e1, e2 = onehot3(p)
        return (
            e0 * X + e1 * Y + e2 * Z,
            e0 * Y + e1 * Z + e2 * X,
            e0 * Z + e1 * X + e2 * Y,
        )

    def slot_of(p, ja, jb, hd):
        e0, e1, e2 = onehot3(p)
        jd = 2 * hd + (C + ja + jb) % 2
        jx = e0 * ja + e1 * jd + e2 * jb
        jy = e0 * jb + e1 * ja + e2 * jd
        jz = e0 * jd + e1 * jb + e2 * ja
        return (jx * 4 + jz) * 2 + jy // 2

    sigma = 1 - 2 * C

    def order(b):
        return [(b + 2) % 4, (b + sigma + 4) % 4, (b - sigma + 4) % 4, b]

    def products(p, ja, b, h):
        wide = [F[slot_of(p, ja, jb, hd)] for hd in (h, 1 - h) for jb in order(b)]
        return jnp.dot(W[p], jnp.concatenate(wide, axis=1), preferred_element_type=F32)

    def settle(buf, at, sem):
        pltpu.make_async_copy(buf.at[at], buf.at[at], sem).wait()

    def send_pair(u, buf, at, half, dst, ssem, rsem):
        at = at + (pl.ds(2 * half, 2),)
        remote(buf.at[at], dst.at[at], ssem, rsem, along(u // 2, 1 - 2 * (u % 2))).start()

    n_piece = (pl.ds(0, 2), 2, 3)

    def send_n(u, hd, m):
        at = (u, hd, n_piece[m])
        remote(
            s_n.at[at], r_n.at[at], sem_sn, sem_n.at[u, hd, m], along(u // 2, 1 - 2 * (u % 2))
        ).start()

    @pl.loop(0, 3)
    def _(v):
        p = (v + C) % 3
        a, b, d = part_coords(p)
        center(p)
        acc[...] = products(p, (a + 2) % 4, b, 0)

        def put(g, i, tile):
            s_far[2 * p + i // 4, i % 4, rows(g), :] = tile

        encode(lambda g: acc[rows(g), :], put, 1024)
        for half in range(2):
            for hd in range(2):
                u = 2 * p + hd
                send_pair(u, s_far, (u,), half, r_far, sem_sfar, sem_far.at[u, half])

    cell_sums((1 - C) * T_DEV, False)
    tb1[...] = jnp.zeros((24, 128), F32)
    ones = jnp.ones((8, KP), BF)
    for p in range(3):
        t = lax.dot_general(ones, W[p], (((1,), (1,)), ((), ())), preferred_element_type=F32)
        tb1[16 + 2 * p : 17 + 2 * p, :] = t[0:1, 0:128]
        tb1[17 + 2 * p : 18 + 2 * p, 0:80] = t[0:1, 128:208]

    def gather_sums(dst, ja):
        for jb in range(4):
            for hd in range(2):
                s = slot_of(0, ja, jb, hd)
                i = 2 * jb + hd
                dst[i : i + 1, :] = fsum[s, 0:1, :]
                dst[8 + i : 9 + i, :] = fsum[s, 1:2, :]

    gather_sums(tb1, X)
    sxc = []
    for d in range(1, 4):
        to = sx_s.at[d - 1]
        to[16:24, :] = tb1[16:24, :]
        gather_sums(to, (X + d) % 4)
        c = remote(to, sx_r.at[d - 1], sem_ss.at[d - 1], sem_sr.at[d - 1], peer(dx=d))
        c.start()
        sxc.append(c)

    @pl.loop(0, 6)
    def _(v):
        u = (v + 2 * C) % 6
        p, dr = u // 2, u % 2
        a, b, d = part_coords(p)
        got = products(p, (a + 1 - 2 * dr + 4) % 4, b, 1 - dr)
        acc[:, 0:512] = got[:, 0:512]
        for i in range(4):
            NP[u, i] = got[:, 512 + 128 * i : 640 + 128 * i]

        def put(g, i, tile):
            s_n[u, 1 - dr, i, rows(g), :] = tile

        encode(lambda g: acc[rows(g), 0:512], put, 512)
        send_n(u, 1 - dr, 0)

    def near_half(half):
        @pl.loop(0, 6)
        def _(v):
            u = (v + 2 * C) % 6
            p, dr = u // 2, u % 2
            if half:
                send_n(u, 1 - dr, 1)
            settle(r_far, (u, pl.ds(2 * half, 2)), sem_far.at[u, half])
            for i in (2 * half, 2 * half + 1):
                got = decode(lambda g: r_far[u, i, rows(g), :])
                for g in range(G):
                    acc[rows(g), 128 * (i % 2) : 128 * (i % 2) + 128] = (
                        NP[u, i, rows(g), :] + got[g]
                    )

            def put(g, i, tile):
                s_n[u, dr, 2 * half + i, rows(g), :] = tile

            encode(lambda g: acc[rows(g), 0:256], put, 256)
            send_n(u, dr, half)
            if half:
                send_n(u, 1 - dr, 2)

    near_half(0)

    @pl.loop(0, 3)
    def _(p):
        a, b, d = part_coords(p)
        got = products(p, a, b, 0)
        for hd in range(2):
            for i in range(4):
                at = 512 * hd + 128 * i
                S1[2 * p + hd, i] = got[:, at : at + 128]

    near_half(1)

    for c in sxc:
        c.wait_recv()
    tb1[...] = (tb1[...] + sx_r[0]) + (sx_r[1] + sx_r[2])
    syc = [
        remote(tb1, sy_r.at[d - 1], sem_ss.at[2 + d], sem_sr.at[2 + d], peer(dy=d))
        for d in range(1, 4)
    ]
    for c in syc:
        c.start()

    def add_tile(w, i, *coded):
        got = [decode(lambda g, c=c: c(g)) for c in coded]
        for g in range(G):
            one = S1[w, i, rows(g), :]
            for c in got:
                one = one + c[g]
            S1[w, i, rows(g), :] = one

    def arrived(w, m):
        p, hd = w // 2, w % 2
        for dr in (1 - hd, hd):
            u = 2 * p + dr
            settle(r_n, (u, hd, n_piece[m]), sem_n.at[u, hd, m])
        for i in ((0, 1), (2,), (3,))[m]:
            add_tile(
                w, i,
                lambda g: r_n[2 * p, hd, i, rows(g), :],
                lambda g: r_n[2 * p + 1, hd, i, rows(g), :],
            )

    def encode1(w, i, buf, at):
        def put(g, t, tile):
            buf[at + (rows(g), slice(None))] = tile

        encode(lambda g: S1[w, i, rows(g), :], put, 128)

    @pl.loop(0, 6)
    def _(v):
        u = (v + 3 * C) % 6
        arrived(u, 0)
        encode1(u, 0, s2f, (u,))
        remote(
            s2f.at[u], r2f.at[u], sem_s2f, sem_2f.at[u],
            along((u // 2 + 1) % 3, 1 - 2 * (u % 2)),
        ).start()

    def near2(p, i, dr, hd):
        u = 2 * p + dr
        encode1(2 * p + hd, i, s2n, (u, hd))
        remote(
            s2n.at[u, hd], r2n.at[u, hd], sem_s2n, sem_2n.at[u, hd],
            along((p + 1) % 3, 1 - 2 * dr),
        ).start()

    def near2_sum(p, i, dr):
        u = 2 * p + dr
        settle(r2f, (u,), sem_2f.at[u])
        add_tile(u, i, lambda g: r2f[u, rows(g), :])
        near2(p, i, dr, dr)

    @pl.loop(0, 3)
    def _(p):
        near2(p, 1, C, 1 - C)

    @pl.loop(0, 6)
    def _(v):
        u = (v + 2 * C) % 6
        send_n(u, u % 2, 2)

    for c in syc:
        c.wait_recv()
    tb2[...] = (tb1[...] + sy_r[0]) + (sy_r[1] + sy_r[2])
    szc = [
        remote(tb2, sz_r.at[d - 1], sem_ss.at[5 + d], sem_sr.at[5 + d], peer(dz=d))
        for d in range(1, 4)
    ]
    for c in szc:
        c.start()

    @pl.loop(0, 3)
    def _(p):
        near2_sum(p, 1, C)

    @pl.loop(0, 3)
    def _(p):
        arrived(2 * p + C, 1)
        near2(p, 2, 1 - C, C)

    @pl.loop(0, 3)
    def _(p):
        arrived(2 * p + 1 - C, 1)
        near2_sum(p, 2, 1 - C)

    @pl.loop(0, 6)
    def _(w):
        arrived(w, 2)

    final = (C + X + Y + Z) % 2 == 0
    lane16 = lax.broadcasted_iota(I32, (16, 128), 1)

    @pl.loop(0, 3)
    def _(p):
        a, b, d = part_coords(p)
        for hd in range(2):
            w = 2 * p + hd
            settle(r2n, (2 * p + 1 - hd, hd), sem_2n.at[2 * p + 1 - hd, hd])
            settle(r2n, (2 * p + hd, hd), sem_2n.at[2 * p + hd, hd])
            add_tile(
                w, 3,
                lambda g: r2n[2 * p, hd, rows(g), :],
                lambda g: r2n[2 * p + 1, hd, rows(g), :],
            )

        def last_send(w, i, delta):
            raw = []
            encode(lambda g: S1[w, 3, rows(g), :], None, 128, raw)
            for h in range(2):
                for g, q in enumerate(fold(raw, h, lane16)):
                    s3[p, i, h, rows(g), :] = q.astype(I32).astype(jnp.int16)
                remote(
                    s3.at[p, i, h], r3.at[p, i], sem_s3.at[h], sem_3.at[p, i],
                    along((p + 2) % 3, delta, (h + C) % 2),
                ).start()

        @pl.when(final)
        def _():
            last_send(2 * p + 1 - d // 2, 2, 2)
            chunks = [S1[2 * p + d // 2, 3, rows(g), :] for g in range(G)]
            two = [fold(chunks, h, lane16) for h in range(2)]
            for g in range(HG):
                fin[p, rows(g), :] = jnp.where(C == 0, two[0][g], two[1][g])
                bs[p, rows(g), :] = jnp.where(C == 0, two[1][g], two[0][g])
            remote(bs.at[p], fin.at[p], sem_bs, sem_br.at[p], partner).start()

        @pl.when(jnp.logical_not(final))
        def _():
            for i, delta in enumerate((1, 3)):
                last_send(2 * p + ((d + delta) % 4) // 2, i, delta)

    for c in szc:
        c.wait_recv()
    total = (tb2[...] + sz_r[0]) + (sz_r[1] + sz_r[2])
    tot_o[...] = total[16:24, :]

    @pl.when(final)
    def _():
        i = 2 * Y + Z // 2
        tb3[...] = total
        sums_o[...] = jnp.zeros((8, 128), F32)
        sums_o[0:1, :] = tb3[pl.ds(i, 1), :]
        sums_o[1:2, :] = tb3[pl.ds(i + 8, 1), :]
        remote(sums_o, sums_o, sem_os, sem_or, partner).start()

    @pl.loop(0, 3)
    def _(p):
        @pl.when(jnp.logical_not(final))
        def _():
            settle(fin, (p,), sem_br.at[p])

        got = []
        for i in range(3):
            settle(r3, (p, i), sem_3.at[p, i])
            got.append(decode_folded(lambda g: r3[p, i, rows(g), :]))
        for g in range(HG):
            fin[p, rows(g), :] = (fin[p, rows(g), :] + got[0][g]) + (got[1][g] + got[2][g])

    @pl.when(final)
    def _():
        pltpu.make_async_copy(bs, bs, sem_bs).wait()
        pltpu.make_async_copy(sums_o, sums_o, sem_os).wait()
        for h in range(2):
            pltpu.make_async_copy(s3.at[:, 2, h], s3.at[:, 2, h], sem_s3.at[h]).wait()

    @pl.when(jnp.logical_not(final))
    def _():
        pltpu.make_async_copy(sums_o, sums_o, sem_or).wait()
        for h in range(2):
            pltpu.make_async_copy(s3.at[:, 0:2, h], s3.at[:, 0:2, h], sem_s3.at[h]).wait()

    for c in g1c + g2c + iwc + sxc + syc + szc:
        c.wait_send()
    pltpu.make_async_copy(F.at[:, own_days, :], F.at[:, own_days, :], sem_fs).wait()
    for buf, sem in ((s_far, sem_sfar), (s_n, sem_sn), (s2f, sem_s2f), (s2n, sem_s2n)):
        pltpu.make_async_copy(buf, buf, sem).wait()


def last_kernel(fin, sums, tot, stat, lag_list, mask, out, WS):
    core = lax.axis_index("core")
    n = float(TDAYS)
    half = 16 * HG
    both = sums[0:8, :]
    turned = pltpu.roll(both, 64, axis=1)
    low = lax.broadcasted_iota(I32, (8, 128), 1) < 64
    both = jnp.where(low == (core == 0), both, turned)
    mean_x = both[0:1, :] / n
    var_x = both[1:2, :] / n - mean_x * mean_x
    inv = 1.0 / (n * jnp.sqrt(var_x + 1e-6))
    row = lax.broadcasted_iota(I32, (half, 256), 0)
    col = lax.broadcasted_iota(I32, (half, 256), 1)
    left = lax.broadcasted_iota(I32, (half, 128), 1) < 64
    WS[KC * LAGS - 2 : KC * LAGS + 6, :] = jnp.zeros((8, 128), F32)
    for p in range(3):
        t = jnp.concatenate([tot[2 * p : 2 * p + 1, :], tot[2 * p + 1 : 2 * p + 2, :]], axis=1)
        t0 = jnp.sum(jnp.where(row == col, t, 0.0), axis=1, keepdims=True)
        t1 = jnp.sum(jnp.where(row + half == col, t, 0.0), axis=1, keepdims=True)
        x = (fin[p] - mean_x * jnp.where(left, t0, t1)) * inv
        m = min(PR, KC * LAGS - PR * p)
        WS[PR * p : PR * p + half, 0:64] = x[:, 0:64]
        WS[PR * p + half : PR * p + m, 0:64] = x[: m - half, 64:128]
    inv_i = 1.0 / jnp.sqrt(stat[1:2, :] + 1e-6)
    lags = lag_list[...].reshape(1, LAGS)
    place = lax.broadcasted_iota(I32, (64, LAGS), 0) - MAXLAG
    pick = (place == lags).astype(F32).astype(BF)
    pick = jnp.concatenate([pick, pick, pick], axis=0)
    r64 = lax.broadcasted_iota(I32, (64, 64), 0)
    c64 = lax.broadcasted_iota(I32, (64, 64), 1)
    sea = mask[...].reshape(1, 64).astype(F32)
    sea = jnp.sum(jnp.where(r64 == c64, sea, 0.0), axis=1, keepdims=True)
    for k in range(KC):
        x = WS[LAGS * k : LAGS * k + 64, 0:64]
        hi = x.astype(BF)
        x = x - hi.astype(F32)
        mid = x.astype(BF)
        lo = (x - mid.astype(F32)).astype(BF)
        y = lax.dot_general(
            jnp.concatenate([hi, mid, lo], axis=0), pick, (((0,), (0,)), ((), ())),
            preferred_element_type=F32,
        )
        out[k] = y * inv_i[:, k : k + 1] * sea


def shards(field, index, lag_list, index_offset, sea_mask):
    vmem = pl.BlockSpec(memory_space=pltpu.VMEM)
    i16 = jnp.int16
    dma = pltpu.SemaphoreType.DMA
    fin, sums, tot, stat = pl.pallas_call(
        main_kernel,
        out_shape=(
            jax.ShapeDtypeStruct((3, 16 * HG, 128), F32),
            jax.ShapeDtypeStruct((8, 128), F32),
            jax.ShapeDtypeStruct((8, 128), F32),
            jax.ShapeDtypeStruct((8, 128), F32),
        ),
        in_specs=[pl.BlockSpec(memory_space=pltpu.HBM)] * 3,
        out_specs=(vmem, vmem, vmem, vmem),
        scratch_shapes=[
            pltpu.VMEM((KC, T_DEV), F32),
            pltpu.SMEM((KC,), I32),
            dma((2,)),
            pltpu.VMEM((32, KP, 128), BF),
            pltpu.VMEM((3, R, KP), BF),
            pltpu.VMEM((3, R, KP), F32),
            pltpu.VMEM((3, R, 128), F32),
            pltpu.VMEM((R, 1024), F32),
            pltpu.VMEM((6, 4, R, 128), F32),
            pltpu.VMEM((6, 4, R, 128), F32),
            pltpu.VMEM((6, 4, R, 128), i16),
            pltpu.VMEM((6, 4, R, 128), i16),
            pltpu.VMEM((6, 2, 4, R, 128), i16),
            pltpu.VMEM((6, 2, 4, R, 128), i16),
            pltpu.VMEM((6, R, 128), i16),
            pltpu.VMEM((6, R, 128), i16),
            pltpu.VMEM((6, 2, R, 128), i16),
            pltpu.VMEM((6, 2, R, 128), i16),
            pltpu.VMEM((3, 3, 2, 16 * HG, 128), i16),
            pltpu.VMEM((3, 3, 16 * HG, 128), i16),
            pltpu.VMEM((3, KC, T_DEV), F32),
            pltpu.VMEM((4, 16, 384), F32),
            pltpu.VMEM((3, 16 * HG, 128), F32),
            pltpu.VMEM((8, 2, 128), F32),
            pltpu.VMEM((16, 2, 128), F32),
            pltpu.VMEM((32, 8, 128), F32),
            pltpu.VMEM((3, 24, 128), F32),
            pltpu.VMEM((3, 24, 128), F32),
            pltpu.VMEM((24, 128), F32),
            pltpu.VMEM((3, 24, 128), F32),
            pltpu.VMEM((24, 128), F32),
            pltpu.VMEM((3, 24, 128), F32),
            pltpu.VMEM((24, 128), F32),
            dma,
            dma,
            dma,
            dma((3,)),
            dma((3,)),
            dma((22,)),
            dma((7,)),
            dma((15,)),
            dma((6, 2)),
            dma((6, 2, 3)),
            dma((6,)),
            dma((6, 2)),
            dma((3, 3)),
            dma,
            dma,
            dma,
            dma,
            dma((2,)),
            dma((9,)),
            dma((9,)),
            dma,
            dma,
            dma,
            dma((3,)),
        ],
        compiler_params=pltpu.CompilerParams(
            collective_id=0, has_side_effects=True, vmem_limit_bytes=36 * 1024 * 1024
        ),
    )(*(pltpu.with_memory_space_constraint(v, pltpu.HBM) for v in (field, index.T, index_offset)))
    maps = pl.pallas_call(
        last_kernel,
        out_shape=jax.ShapeDtypeStruct((KC, CELLS // 128, LAGS), F32),
        in_specs=[vmem] * 6,
        out_specs=vmem,
        scratch_shapes=[pltpu.VMEM((616, 128), F32)],
        compiler_params=pltpu.CompilerParams(vmem_limit_bytes=8 * 1024 * 1024),
    )(fin, sums, tot, stat, lag_list, sea_mask)
    return jnp.transpose(maps, (1, 0, 2))


def solution(mesh):
    finer = Mesh(mesh.devices.reshape(4, 4, 4, 2), TM)
    return jax.shard_map(
        shards,
        mesh=finer,
        in_specs=(P(TM, None), P(TM, None), P(), P(), P(TM)),
        out_specs=P(TM, None, None),
        check_vma=False,
    )
```

profile of v0, /device:TPU:1, one launch (start us, length us, event | category | flops | bytes accessed | tf_op | source)
XLA Modules:
  0.0 47.8 jit_solution(389367101915739575)
XLA Ops:
  0.0 0.0 copy-start.1
  0.0 0.0 copy-start
  0.0 46.4 %shard_map.55 = (f32[3,112,128]{2,1,0:T(8,128)S(1)}, f32[8,128]{1,0:T(8,128)S(1)}, f32[8,128]{1,0:T(8,128)S(1)}, f32[8,128]{1,0:T(8,128)S(1)}) custom-call(bf16[336,8192]{1,0:T(8,128)(2,1)} %field.1, f32[10,336]{1,0:T(8,128)} %bitcast.2, s32[10]{0:T(128)} %offs_in.1), custom_call_target="tpu_custom_call" | custom-call | tf_op jit(solution)/shard_map/pallas_call | solution.py:698
  46.4 0.0 copy-done.1
  46.4 0.0 copy-done
  46.4 1.4 %shard_map.56 = f32[10,64,61]{2,1,0:T(8,128)} custom-call(f32[3,112,128]{2,1,0:T(8,128)S(1)} %get-tuple-element.9.fin, f32[8,128]{1,0:T(8,128)S(1)} %get-tuple-element.10.sums, f32[8,128]{1,0:T(8,128)S(1)} %get-tuple-element.11.tot, f32[8,128]{1,0:T(8,128)S(1)} %get-tuple-element.12.stat, s32[61]{0:T(128)S(1)} %copy-done, s32[64]{0:T(128)S(1)} %copy-done.1), custom_call_target="tpu_custom_call" | custom-call | tf_op jit(solution)/shard_map/pallas_call | solution.py:771
Async XLA Ops:
  0.0 46.4 %copy-start.1 = (s32[64]{0:T(128)S(1)}, s32[64]{0:T(128)}, u32[]{:S(2)}) copy-start(s32[64]{0:T(128)} %mask.1) | copy-start | bytes 772
  0.0 46.4 %copy-start = (s32[61]{0:T(128)S(1)}, s32[61]{0:T(128)}, u32[]{:S(2)}) copy-start(s32[61]{0:T(128)} %lag_list.1) | copy-start | bytes 736
where the time goes:
time: 48 us; the launch traced here: 47.8 us
  Pallas kernels  47.8 us (100%)
    pallas_call x1, Pallas kernels, shards(): pl.pallas_call(main_kernel, out_shape=(jax.ShapeDtypeStruct((3, 16 * HG,...  46.4 us
    pallas_call x1, Pallas kernels, shards(): pl.pallas_call(last_kernel, out_shape=jax.ShapeDtypeStruct((KC, CELLS //...  1.4 us

commit v1 on v0

--- a/solution.py
+++ b/solution.py
@@ -109,7 +109,7 @@
     field, idx_in, offs_in, fin, sums_o, tot_o, stat_o,
     idx, offs, sem_in, F, W, WF, OH, acc, NP, S1,
     s_far, r_far, s_n, r_n, s2f, r2f, s2n, r2n, s3, r3,
-    iw, ipad, bs, g1, g2, fsum, sx_s, sx_r, tb1, sy_r, tb2, sz_r, tb3,
+    iw, ipad, bs, g1, g2, fsum, sx_s, sx_r, tb1, sy_s, sy_r, tb3,
     sem_loc, sem_fs, sem_fr, sem_is, sem_ir, sem_gs, sem_g1, sem_g2,
     sem_far, sem_n, sem_2f, sem_2n, sem_3,
     sem_sfar, sem_sn, sem_s2f, sem_s2n, sem_s3, sem_ss, sem_sr, sem_os, sem_or, sem_bs, sem_br,
@@ -190,18 +190,21 @@
             device_id=device, device_id_type=MESH,
         )
 
+    def settle(buf, at, sem):
+        pltpu.make_async_copy(buf.at[at], buf.at[at], sem).wait()
+
     g1c = [
-        remote(g1.at[me8], g1.at[me8], sem_gs.at[i], sem_g1.at[i], peer(dx=dx, dc=dc))
-        for i, (dx, dc) in enumerate(xpeers)
+        remote(g1.at[me8], g1.at[me8], sem_gs.at[0], sem_g1, peer(dx=dx, dc=dc))
+        for dx, dc in xpeers
     ]
     for c in g1c:
         c.start()
     beside = (Q + N_CHIP + 2 * C - 1) % N_CHIP
-    iwc = [remote(idx, iw.at[2], sem_is.at[2], sem_ir.at[2], partner)]
+    iwc = [remote(idx, iw.at[2], sem_is, sem_ir, partner)]
     for core in range(2):
         iwc.append(
             remote(
-                idx, iw.at[1 - C], sem_is.at[core], sem_ir.at[1 - C], chip_peer(beside, core)
+                idx, iw.at[1 - C], sem_is, sem_ir, chip_peer(beside, core)
             )
         )
     for c in iwc:
@@ -230,38 +233,32 @@
         ipad[i] = jnp.zeros((16, 384), F32)
     ipad[3, 0:KC, 0:T_DEV] = mine
 
-    for c in g1c:
-        c.wait_recv()
+    settle(g1, (pl.ds(0, 7),), sem_g1)
     g = ((g1[0] + g1[1]) + (g1[2] + g1[3])) + ((g1[4] + g1[5]) + (g1[6] + g1[7]))
     g2[me16] = g
     g2c = [
         remote(
-            g2.at[me16], g2.at[me16], sem_gs.at[7 + i], sem_g2.at[i], peer(dy=dy, dz=dz)
+            g2.at[me16], g2.at[me16], sem_gs.at[1], sem_g2, peer(dy=dy, dz=dz)
         )
-        for i, (dy, dz) in enumerate(yzpeers)
+        for dy, dz in yzpeers
     ]
     for c in g2c:
         c.start()
     share(10, 32)
 
-    def cell_sums(start, fresh):
+    def cell_sums():
         @pl.loop(0, 32)
         def _(s):
             one = two = jnp.zeros((16, 128), F32)
-            for g in range(T_DEV // 16):
-                v = F[s, pl.ds(pl.multiple_of(start + 16 * g, 16), 16), :].astype(F32)
+            for g in range(K // 16):
+                v = F[s, rows(g), :].astype(F32)
                 one, two = one + v, two + v * v
-            one = jnp.sum(one, axis=0, keepdims=True)
-            two = jnp.sum(two, axis=0, keepdims=True)
-            if not fresh:
-                one, two = one + fsum[s, 0:1, :], two + fsum[s, 1:2, :]
-            fsum[s, 0:1, :] = one
-            fsum[s, 1:2, :] = two
+            fsum[s, 0:1, :] = jnp.sum(one, axis=0, keepdims=True)
+            fsum[s, 1:2, :] = jnp.sum(two, axis=0, keepdims=True)
 
     pltpu.make_async_copy(F.at[:, own_days, :], F.at[:, own_days, :], sem_loc).wait()
-    cell_sums(C * T_DEV, True)
+    pltpu.make_async_copy(iw, iw, sem_ir).wait()
     for i in range(3):
-        pltpu.make_async_copy(iw.at[i], iw.at[i], sem_ir.at[i]).wait()
         ipad[i, 0:KC, 0:T_DEV] = iw[i]
     pos = lax.broadcasted_iota(I32, (16, LC), 1)
 
@@ -307,8 +304,7 @@
             if kk == k:
                 WF[p, b : b + n, :] = x[a : a + n, :]
 
-    for c in g2c:
-        c.wait_recv()
+    settle(g2, (pl.ds(0, 15),), sem_g2)
     g = g2[0]
     for i in range(1, 16):
         g = g + g2[i]
@@ -351,20 +347,21 @@
         wide = [F[slot_of(p, ja, jb, hd)] for hd in (h, 1 - h) for jb in order(b)]
         return jnp.dot(W[p], jnp.concatenate(wide, axis=1), preferred_element_type=F32)
 
-    def settle(buf, at, sem):
-        pltpu.make_async_copy(buf.at[at], buf.at[at], sem).wait()
-
-    def send_pair(u, buf, at, half, dst, ssem, rsem):
-        at = at + (pl.ds(2 * half, 2),)
-        remote(buf.at[at], dst.at[at], ssem, rsem, along(u // 2, 1 - 2 * (u % 2))).start()
-
-    n_piece = (pl.ds(0, 2), 2, 3)
-
     def send_n(u, hd, m):
-        at = (u, hd, n_piece[m])
+        at = (u, hd, m)
         remote(
-            s_n.at[at], r_n.at[at], sem_sn, sem_n.at[u, hd, m], along(u // 2, 1 - 2 * (u % 2))
+            s_n.at[at], r_n.at[at], sem_sn, sem_n.at[u // 2, hd, m], along(u // 2, 1 - 2 * (u % 2))
         ).start()
+
+    def send_far(u, m):
+        at = (u, m)
+        remote(
+            s_far.at[at], r_far.at[at], sem_sfar, sem_far.at[u, m],
+            along(u // 2, 1 - 2 * (u % 2)),
+        ).start()
+
+    def turn(v):
+        return v + C * (5 - 2 * v)
 
     @pl.loop(0, 3)
     def _(v):
@@ -377,40 +374,13 @@
             s_far[2 * p + i // 4, i % 4, rows(g), :] = tile
 
         encode(lambda g: acc[rows(g), :], put, 1024)
-        for half in range(2):
-            for hd in range(2):
-                u = 2 * p + hd
-                send_pair(u, s_far, (u,), half, r_far, sem_sfar, sem_far.at[u, half])
-
-    cell_sums((1 - C) * T_DEV, False)
-    tb1[...] = jnp.zeros((24, 128), F32)
-    ones = jnp.ones((8, KP), BF)
-    for p in range(3):
-        t = lax.dot_general(ones, W[p], (((1,), (1,)), ((), ())), preferred_element_type=F32)
-        tb1[16 + 2 * p : 17 + 2 * p, :] = t[0:1, 0:128]
-        tb1[17 + 2 * p : 18 + 2 * p, 0:80] = t[0:1, 128:208]
-
-    def gather_sums(dst, ja):
-        for jb in range(4):
-            for hd in range(2):
-                s = slot_of(0, ja, jb, hd)
-                i = 2 * jb + hd
-                dst[i : i + 1, :] = fsum[s, 0:1, :]
-                dst[8 + i : 9 + i, :] = fsum[s, 1:2, :]
-
-    gather_sums(tb1, X)
-    sxc = []
-    for d in range(1, 4):
-        to = sx_s.at[d - 1]
-        to[16:24, :] = tb1[16:24, :]
-        gather_sums(to, (X + d) % 4)
-        c = remote(to, sx_r.at[d - 1], sem_ss.at[d - 1], sem_sr.at[d - 1], peer(dx=d))
-        c.start()
-        sxc.append(c)
+        for hd in range(2):
+            for i in range(3):
+                send_far(2 * p + hd, i)
 
     @pl.loop(0, 6)
     def _(v):
-        u = (v + 2 * C) % 6
+        u = turn(v)
         p, dr = u // 2, u % 2
         a, b, d = part_coords(p)
         got = products(p, (a + 1 - 2 * dr + 4) % 4, b, 1 - dr)
@@ -423,31 +393,30 @@
 
         encode(lambda g: acc[rows(g), 0:512], put, 512)
         send_n(u, 1 - dr, 0)
-
-    def near_half(half):
+        send_n(u, 1 - dr, 1)
+
+    def near_sum(i):
         @pl.loop(0, 6)
         def _(v):
-            u = (v + 2 * C) % 6
-            p, dr = u // 2, u % 2
-            if half:
-                send_n(u, 1 - dr, 1)
-            settle(r_far, (u, pl.ds(2 * half, 2)), sem_far.at[u, half])
-            for i in (2 * half, 2 * half + 1):
-                got = decode(lambda g: r_far[u, i, rows(g), :])
-                for g in range(G):
-                    acc[rows(g), 128 * (i % 2) : 128 * (i % 2) + 128] = (
-                        NP[u, i, rows(g), :] + got[g]
-                    )
-
-            def put(g, i, tile):
-                s_n[u, dr, 2 * half + i, rows(g), :] = tile
-
-            encode(lambda g: acc[rows(g), 0:256], put, 256)
-            send_n(u, dr, half)
-            if half:
-                send_n(u, 1 - dr, 2)
-
-    near_half(0)
+            u = turn(v)
+            dr = u % 2
+            settle(r_far, (u, i), sem_far.at[u, i])
+            got = decode(lambda g: r_far[u, i, rows(g), :])
+            for g in range(G):
+                acc[rows(g), 0:128] = NP[u, i, rows(g), :] + got[g]
+
+            def put(g, t, tile):
+                s_n[u, dr, i, rows(g), :] = tile
+
+            encode(lambda g: acc[rows(g), 0:128], put, 128)
+            send_n(u, dr, i)
+            if i == 0:
+                send_far(u, 3)
+            if 0 < i < 3:
+                send_n(u, 1 - dr, i + 1)
+
+    near_sum(0)
+    near_sum(1)
 
     @pl.loop(0, 3)
     def _(p):
@@ -458,18 +427,6 @@
                 at = 512 * hd + 128 * i
                 S1[2 * p + hd, i] = got[:, at : at + 128]
 
-    near_half(1)
-
-    for c in sxc:
-        c.wait_recv()
-    tb1[...] = (tb1[...] + sx_r[0]) + (sx_r[1] + sx_r[2])
-    syc = [
-        remote(tb1, sy_r.at[d - 1], sem_ss.at[2 + d], sem_sr.at[2 + d], peer(dy=d))
-        for d in range(1, 4)
-    ]
-    for c in syc:
-        c.start()
-
     def add_tile(w, i, *coded):
         got = [decode(lambda g, c=c: c(g)) for c in coded]
         for g in range(G):
@@ -478,23 +435,44 @@
                 one = one + c[g]
             S1[w, i, rows(g), :] = one
 
-    def arrived(w, m):
+    def arrived(w, i):
         p, hd = w // 2, w % 2
-        for dr in (1 - hd, hd):
-            u = 2 * p + dr
-            settle(r_n, (u, hd, n_piece[m]), sem_n.at[u, hd, m])
-        for i in ((0, 1), (2,), (3,))[m]:
-            add_tile(
-                w, i,
-                lambda g: r_n[2 * p, hd, i, rows(g), :],
-                lambda g: r_n[2 * p + 1, hd, i, rows(g), :],
-            )
+        settle(r_n, (pl.ds(2 * p, 2), hd, i), sem_n.at[p, hd, i])
+        add_tile(
+            w, i,
+            lambda g: r_n[2 * p, hd, i, rows(g), :],
+            lambda g: r_n[2 * p + 1, hd, i, rows(g), :],
+        )
 
     def encode1(w, i, buf, at):
         def put(g, t, tile):
             buf[at + (rows(g), slice(None))] = tile
 
         encode(lambda g: S1[w, i, rows(g), :], put, 128)
+
+    cell_sums()
+    tb1[...] = jnp.zeros((24, 128), F32)
+    ones = jnp.ones((8, KP), BF)
+    for p in range(3):
+        t = lax.dot_general(ones, W[p], (((1,), (1,)), ((), ())), preferred_element_type=F32)
+        tb1[16 + 2 * p : 17 + 2 * p, :] = t[0:1, 0:128]
+        tb1[17 + 2 * p : 18 + 2 * p, 0:80] = t[0:1, 128:208]
+
+    def gather_sums(dst, ja):
+        for jb in range(4):
+            for hd in range(2):
+                s = slot_of(0, ja, jb, hd)
+                i = 2 * jb + hd
+                dst[i : i + 1, :] = fsum[s, 0:1, :]
+                dst[8 + i : 9 + i, :] = fsum[s, 1:2, :]
+
+    gather_sums(tb1, X)
+    for d in range(1, 4):
+        to = sx_s.at[d - 1]
+        to[16:24, :] = tb1[16:24, :]
+        gather_sums(to, (X + d) % 4)
+        c = remote(to, sx_r.at[d - 1], sem_ss.at[0], sem_sr.at[0], peer(dx=d))
+        c.start()
 
     @pl.loop(0, 6)
     def _(v):
@@ -510,7 +488,7 @@
         u = 2 * p + dr
         encode1(2 * p + hd, i, s2n, (u, hd))
         remote(
-            s2n.at[u, hd], r2n.at[u, hd], sem_s2n, sem_2n.at[u, hd],
+            s2n.at[u, hd], r2n.at[u, hd], sem_s2n, sem_2n.at[p, hd],
             along((p + 1) % 3, 1 - 2 * dr),
         ).start()
 
@@ -520,42 +498,48 @@
         add_tile(u, i, lambda g: r2f[u, rows(g), :])
         near2(p, i, dr, dr)
 
+    near_sum(2)
+    near_sum(3)
+
     @pl.loop(0, 3)
     def _(p):
+        arrived(2 * p + 1 - C, 1)
         near2(p, 1, C, 1 - C)
-
-    @pl.loop(0, 6)
-    def _(v):
-        u = (v + 2 * C) % 6
-        send_n(u, u % 2, 2)
-
-    for c in syc:
-        c.wait_recv()
-    tb2[...] = (tb1[...] + sy_r[0]) + (sy_r[1] + sy_r[2])
-    szc = [
-        remote(tb2, sz_r.at[d - 1], sem_ss.at[5 + d], sem_sr.at[5 + d], peer(dz=d))
-        for d in range(1, 4)
-    ]
-    for c in szc:
-        c.start()
-
-    @pl.loop(0, 3)
-    def _(p):
-        near2_sum(p, 1, C)
 
     @pl.loop(0, 3)
     def _(p):
         arrived(2 * p + C, 1)
-        near2(p, 2, 1 - C, C)
+        near2_sum(p, 1, C)
+
+    pltpu.make_async_copy(sx_r, sx_r, sem_sr.at[0]).wait()
+    tb1[...] = (tb1[...] + sx_r[0]) + (sx_r[1] + sx_r[2])
+
+    def side_rows(dst, y, z):
+        i = 2 * y + z // 2
+        dst[0:1, :] = tb1[pl.ds(i, 1), :]
+        dst[1:2, :] = tb1[pl.ds(8 + i, 1), :]
+        dst[2:8, :] = tb1[16:22, :]
+
+    for n, (dy, dz) in enumerate(yzpeers):
+        side_rows(sy_s.at[n], (Y + dy) % 4, (Z + dz) % 4)
+        c = remote(
+            sy_s.at[n], sy_r.at[n], sem_ss.at[1], sem_sr.at[1], peer(dy=dy, dz=dz)
+        )
+        c.start()
 
     @pl.loop(0, 3)
     def _(p):
-        arrived(2 * p + 1 - C, 1)
+        arrived(2 * p + C, 2)
+        near2(p, 2, 1 - C, C)
+
+    @pl.loop(0, 3)
+    def _(p):
+        arrived(2 * p + 1 - C, 2)
         near2_sum(p, 2, 1 - C)
 
     @pl.loop(0, 6)
     def _(w):
-        arrived(w, 2)
+        arrived(w, 3)
 
     final = (C + X + Y + Z) % 2 == 0
     lane16 = lax.broadcasted_iota(I32, (16, 128), 1)
@@ -565,8 +549,7 @@
         a, b, d = part_coords(p)
         for hd in range(2):
             w = 2 * p + hd
-            settle(r2n, (2 * p + 1 - hd, hd), sem_2n.at[2 * p + 1 - hd, hd])
-            settle(r2n, (2 * p + hd, hd), sem_2n.at[2 * p + hd, hd])
+            settle(r2n, (pl.ds(2 * p, 2), hd), sem_2n.at[p, hd])
             add_tile(
                 w, 3,
                 lambda g: r2n[2 * p, hd, rows(g), :],
@@ -580,7 +563,7 @@
                 for g, q in enumerate(fold(raw, h, lane16)):
                     s3[p, i, h, rows(g), :] = q.astype(I32).astype(jnp.int16)
                 remote(
-                    s3.at[p, i, h], r3.at[p, i], sem_s3.at[h], sem_3.at[p, i],
+                    s3.at[p, i, h], r3.at[p, i], sem_s3.at[h], sem_3.at[p],
                     along((p + 2) % 3, delta, (h + C) % 2),
                 ).start()
 
@@ -599,18 +582,16 @@
             for i, delta in enumerate((1, 3)):
                 last_send(2 * p + ((d + delta) % 4) // 2, i, delta)
 
-    for c in szc:
-        c.wait_recv()
-    total = (tb2[...] + sz_r[0]) + (sz_r[1] + sz_r[2])
-    tot_o[...] = total[16:24, :]
+    side_rows(tb3, Y, Z)
+    total = tb3[...]
+    pltpu.make_async_copy(sy_r, sy_r, sem_sr.at[1]).wait()
+    for n in range(15):
+        total = total + sy_r[n]
+    tot_o[...] = total
 
     @pl.when(final)
     def _():
-        i = 2 * Y + Z // 2
-        tb3[...] = total
-        sums_o[...] = jnp.zeros((8, 128), F32)
-        sums_o[0:1, :] = tb3[pl.ds(i, 1), :]
-        sums_o[1:2, :] = tb3[pl.ds(i + 8, 1), :]
+        sums_o[...] = total
         remote(sums_o, sums_o, sem_os, sem_or, partner).start()
 
     @pl.loop(0, 3)
@@ -619,9 +600,9 @@
         def _():
             settle(fin, (p,), sem_br.at[p])
 
+        settle(r3, (p,), sem_3.at[p])
         got = []
         for i in range(3):
-            settle(r3, (p, i), sem_3.at[p, i])
             got.append(decode_folded(lambda g: r3[p, i, rows(g), :]))
         for g in range(HG):
             fin[p, rows(g), :] = (fin[p, rows(g), :] + got[0][g]) + (got[1][g] + got[2][g])
@@ -639,14 +620,17 @@
         for h in range(2):
             pltpu.make_async_copy(s3.at[:, 0:2, h], s3.at[:, 0:2, h], sem_s3.at[h]).wait()
 
-    for c in g1c + g2c + iwc + sxc + syc + szc:
-        c.wait_send()
+    settle(g1, (pl.ds(0, 7),), sem_gs.at[0])
+    settle(g2, (pl.ds(0, 15),), sem_gs.at[1])
+    pltpu.make_async_copy(iw, iw, sem_is).wait()
+    pltpu.make_async_copy(sx_s, sx_s, sem_ss.at[0]).wait()
+    pltpu.make_async_copy(sy_s, sy_s, sem_ss.at[1]).wait()
     pltpu.make_async_copy(F.at[:, own_days, :], F.at[:, own_days, :], sem_fs).wait()
     for buf, sem in ((s_far, sem_sfar), (s_n, sem_sn), (s2f, sem_s2f), (s2n, sem_s2n)):
         pltpu.make_async_copy(buf, buf, sem).wait()
 
 
-def last_kernel(fin, sums, tot, stat, lag_list, mask, out, WS):
+def last_kernel(fin, sums, tot, stat, lag_list, mask, out_hbm, WS, out, sem):
     core = lax.axis_index("core")
     n = float(TDAYS)
     half = 16 * HG
@@ -662,7 +646,7 @@
     left = lax.broadcasted_iota(I32, (half, 128), 1) < 64
     WS[KC * LAGS - 2 : KC * LAGS + 6, :] = jnp.zeros((8, 128), F32)
     for p in range(3):
-        t = jnp.concatenate([tot[2 * p : 2 * p + 1, :], tot[2 * p + 1 : 2 * p + 2, :]], axis=1)
+        t = jnp.concatenate([tot[2 * p + 2 : 2 * p + 3, :], tot[2 * p + 3 : 2 * p + 4, :]], axis=1)
         t0 = jnp.sum(jnp.where(row == col, t, 0.0), axis=1, keepdims=True)
         t1 = jnp.sum(jnp.where(row + half == col, t, 0.0), axis=1, keepdims=True)
         x = (fin[p] - mean_x * jnp.where(left, t0, t1)) * inv
@@ -689,6 +673,9 @@
             preferred_element_type=F32,
         )
         out[k] = y * inv_i[:, k : k + 1] * sea
+        pltpu.make_async_copy(out.at[k], out_hbm.at[k], sem.at[k]).start()
+    for k in range(KC):
+        pltpu.make_async_copy(out.at[k], out_hbm.at[k], sem.at[k]).wait()
 
 
 def shards(field, index, lag_list, index_offset, sea_mask):
@@ -735,30 +722,29 @@
             pltpu.VMEM((3, 24, 128), F32),
             pltpu.VMEM((3, 24, 128), F32),
             pltpu.VMEM((24, 128), F32),
-            pltpu.VMEM((3, 24, 128), F32),
-            pltpu.VMEM((24, 128), F32),
-            pltpu.VMEM((3, 24, 128), F32),
-            pltpu.VMEM((24, 128), F32),
-            dma,
-            dma,
-            dma,
+            pltpu.VMEM((15, 8, 128), F32),
+            pltpu.VMEM((15, 8, 128), F32),
+            pltpu.VMEM((8, 128), F32),
+            dma,
+            dma,
+            dma,
+            dma,
+            dma,
+            dma((2,)),
+            dma,
+            dma,
+            dma((6, 4)),
+            dma((3, 2, 4)),
+            dma((6,)),
+            dma((3, 2)),
             dma((3,)),
-            dma((3,)),
-            dma((22,)),
-            dma((7,)),
-            dma((15,)),
-            dma((6, 2)),
-            dma((6, 2, 3)),
-            dma((6,)),
-            dma((6, 2)),
-            dma((3, 3)),
             dma,
             dma,
             dma,
             dma,
             dma((2,)),
-            dma((9,)),
-            dma((9,)),
+            dma((2,)),
+            dma((2,)),
             dma,
             dma,
             dma,
@@ -772,8 +758,12 @@
         last_kernel,
         out_shape=jax.ShapeDtypeStruct((KC, CELLS // 128, LAGS), F32),
         in_specs=[vmem] * 6,
-        out_specs=vmem,
-        scratch_shapes=[pltpu.VMEM((616, 128), F32)],
+        out_specs=pl.BlockSpec(memory_space=pltpu.HBM),
+        scratch_shapes=[
+            pltpu.VMEM((616, 128), F32),
+            pltpu.VMEM((KC, CELLS // 128, LAGS), F32),
+            dma((KC,)),
+        ],
         compiler_params=pltpu.CompilerParams(vmem_limit_bytes=8 * 1024 * 1024),
     )(fin, sums, tot, stat, lag_list, sea_mask)
     return jnp.transpose(maps, (1, 0, 2))

time: 48 us -> 46.3 us (0.965)
  Pallas kernels: 47.8 us -> 46.1 us
    pallas_call x1, Pallas kernels: 46.4 us -> 44.6 us  [shards(): pl.pallas_call(main_kernel, out_shape=(jax.ShapeDtypeStruct((3, 16 * HG,...]
where the time goes in v1:
time: 46.3 us; the launch traced here: 46.1 us
  Pallas kernels  46.1 us (100%)
    pallas_call x1, Pallas kernels, shards(): pl.pallas_call(main_kernel, out_shape=(jax.ShapeDtypeStruct((3, 16 * HG,...  44.6 us
    pallas_call x1, Pallas kernels, shards(): pl.pallas_call(last_kernel, out_shape=jax.ShapeDtypeStruct((KC, CELLS //...  1.44 us

profile of v1, /device:TPU:1, one launch (start us, length us, event | category | flops | bytes accessed | tf_op | source)
XLA Modules:
  0.0 46.1 jit_solution(6612968861443078576)
XLA Ops:
  0.0 0.0 copy-start.1
  0.0 0.0 copy-start
  0.0 44.6 %shard_map.55 = (f32[3,112,128]{2,1,0:T(8,128)S(1)}, f32[8,128]{1,0:T(8,128)S(1)}, f32[8,128]{1,0:T(8,128)S(1)}, f32[8,128]{1,0:T(8,128)S(1)}) custom-call(bf16[336,8192]{1,0:T(8,128)(2,1)} %field.1, f32[10,336]{1,0:T(8,128)} %bitcast.2, s32[10]{0:T(128)} %offs_in.1), custom_call_target="tpu_custom_call" | custom-call | tf_op jit(solution)/shard_map/pallas_call | solution.py:685
  44.6 0.0 copy-done.1
  44.6 0.0 copy-done
  44.7 1.4 %shard_map.56 = f32[10,64,61]{2,1,0:T(8,128)} custom-call(f32[3,112,128]{2,1,0:T(8,128)S(1)} %get-tuple-element.9.fin, f32[8,128]{1,0:T(8,128)S(1)} %get-tuple-element.10.sums, f32[8,128]{1,0:T(8,128)S(1)} %get-tuple-element.11.tot, f32[8,128]{1,0:T(8,128)S(1)} %get-tuple-element.12.stat, s32[61]{0:T(128)S(1)} %copy-done, s32[64]{0:T(128)S(1)} %copy-done.1), custom_call_target="tpu_custom_call" | custom-call | tf_op jit(solution)/shard_map/pallas_call | solution.py:757
Async XLA Ops:
  0.0 44.6 %copy-start.1 = (s32[64]{0:T(128)S(1)}, s32[64]{0:T(128)}, u32[]{:S(2)}) copy-start(s32[64]{0:T(128)} %mask.1) | copy-start | bytes 772
  0.0 44.6 %copy-start = (s32[61]{0:T(128)S(1)}, s32[61]{0:T(128)}, u32[]{:S(2)}) copy-start(s32[61]{0:T(128)} %lag_list.1) | copy-start | bytes 736

commit v2 on v1

--- a/solution.py
+++ b/solution.py
@@ -223,7 +223,7 @@
             field.at[:, columns(s, C)], F.at[s, own_days, :], sem_loc
         ).start()
 
-    share(0, 10)
+    share(0, 20)
 
     @pl.loop(0, 32)
     def _(s):
@@ -244,7 +244,7 @@
     ]
     for c in g2c:
         c.start()
-    share(10, 32)
+    share(20, 32)
 
     def cell_sums():
         @pl.loop(0, 32)
@@ -350,7 +350,7 @@
     def send_n(u, hd, m):
         at = (u, hd, m)
         remote(
-            s_n.at[at], r_n.at[at], sem_sn, sem_n.at[u // 2, hd, m], along(u // 2, 1 - 2 * (u % 2))
+            s_n.at[at], r_n.at[at], sem_sn, sem_n.at[u // 2, m], along(u // 2, 1 - 2 * (u % 2))
         ).start()
 
     def send_far(u, m):
@@ -435,14 +435,14 @@
                 one = one + c[g]
             S1[w, i, rows(g), :] = one
 
-    def arrived(w, i):
-        p, hd = w // 2, w % 2
-        settle(r_n, (pl.ds(2 * p, 2), hd, i), sem_n.at[p, hd, i])
-        add_tile(
-            w, i,
-            lambda g: r_n[2 * p, hd, i, rows(g), :],
-            lambda g: r_n[2 * p + 1, hd, i, rows(g), :],
-        )
+    def arrived(p, i):
+        settle(r_n, (pl.ds(2 * p, 2), slice(None), i), sem_n.at[p, i])
+        for hd in range(2):
+            add_tile(
+                2 * p + hd, i,
+                lambda g: r_n[2 * p, hd, i, rows(g), :],
+                lambda g: r_n[2 * p + 1, hd, i, rows(g), :],
+            )
 
     def encode1(w, i, buf, at):
         def put(g, t, tile):
@@ -474,21 +474,21 @@
         c = remote(to, sx_r.at[d - 1], sem_ss.at[0], sem_sr.at[0], peer(dx=d))
         c.start()
 
-    @pl.loop(0, 6)
-    def _(v):
-        u = (v + 3 * C) % 6
-        arrived(u, 0)
-        encode1(u, 0, s2f, (u,))
-        remote(
-            s2f.at[u], r2f.at[u], sem_s2f, sem_2f.at[u],
-            along((u // 2 + 1) % 3, 1 - 2 * (u % 2)),
-        ).start()
+    @pl.loop(0, 3)
+    def _(p):
+        arrived(p, 0)
+        for hd in range(2):
+            u = 2 * p + hd
+            encode1(u, 0, s2f, (u,))
+            remote(
+                s2f.at[u], r2f.at[u], sem_s2f, sem_2f.at[u], along((p + 1) % 3, 1 - 2 * hd)
+            ).start()
 
     def near2(p, i, dr, hd):
         u = 2 * p + dr
         encode1(2 * p + hd, i, s2n, (u, hd))
         remote(
-            s2n.at[u, hd], r2n.at[u, hd], sem_s2n, sem_2n.at[p, hd],
+            s2n.at[u, hd], r2n.at[u, hd], sem_s2n, sem_2n.at[p],
             along((p + 1) % 3, 1 - 2 * dr),
         ).start()
 
@@ -503,12 +503,11 @@
 
     @pl.loop(0, 3)
     def _(p):
-        arrived(2 * p + 1 - C, 1)
+        arrived(p, 1)
         near2(p, 1, C, 1 - C)
 
     @pl.loop(0, 3)
     def _(p):
-        arrived(2 * p + C, 1)
         near2_sum(p, 1, C)
 
     pltpu.make_async_copy(sx_r, sx_r, sem_sr.at[0]).wait()
@@ -529,17 +528,16 @@
 
     @pl.loop(0, 3)
     def _(p):
-        arrived(2 * p + C, 2)
+        arrived(p, 2)
         near2(p, 2, 1 - C, C)
 
     @pl.loop(0, 3)
     def _(p):
-        arrived(2 * p + 1 - C, 2)
         near2_sum(p, 2, 1 - C)
 
-    @pl.loop(0, 6)
-    def _(w):
-        arrived(w, 3)
+    @pl.loop(0, 3)
+    def _(p):
+        arrived(p, 3)
 
     final = (C + X + Y + Z) % 2 == 0
     lane16 = lax.broadcasted_iota(I32, (16, 128), 1)
@@ -547,9 +545,9 @@
     @pl.loop(0, 3)
     def _(p):
         a, b, d = part_coords(p)
+        settle(r2n, (pl.ds(2 * p, 2),), sem_2n.at[p])
         for hd in range(2):
             w = 2 * p + hd
-            settle(r2n, (pl.ds(2 * p, 2), hd), sem_2n.at[p, hd])
             add_tile(
                 w, 3,
                 lambda g: r2n[2 * p, hd, rows(g), :],
@@ -644,15 +642,20 @@
     row = lax.broadcasted_iota(I32, (half, 256), 0)
     col = lax.broadcasted_iota(I32, (half, 256), 1)
     left = lax.broadcasted_iota(I32, (half, 128), 1) < 64
-    WS[KC * LAGS - 2 : KC * LAGS + 6, :] = jnp.zeros((8, 128), F32)
+    WS[KC * LAGS - LAGS - 5 : KC * LAGS + 6, :] = jnp.zeros((LAGS + 11, 128), F32)
     for p in range(3):
         t = jnp.concatenate([tot[2 * p + 2 : 2 * p + 3, :], tot[2 * p + 3 : 2 * p + 4, :]], axis=1)
         t0 = jnp.sum(jnp.where(row == col, t, 0.0), axis=1, keepdims=True)
         t1 = jnp.sum(jnp.where(row + half == col, t, 0.0), axis=1, keepdims=True)
         x = (fin[p] - mean_x * jnp.where(left, t0, t1)) * inv
-        m = min(PR, KC * LAGS - PR * p)
-        WS[PR * p : PR * p + half, 0:64] = x[:, 0:64]
-        WS[PR * p + half : PR * p + m, 0:64] = x[: m - half, 64:128]
+        y = pltpu.roll(x, 64, axis=1)
+        m = min(PR, KC * LAGS - PR * p) - half
+        at = PR * p
+        WS[at : at + half, 0:64] = x[:, 0:64]
+        WS[at + half : at + half + m, 0:64] = y[:m, 0:64]
+        cut = max(0, LAGS - at)
+        WS[at - LAGS + cut : at - LAGS + half, 64:128] = y[cut:, 64:128]
+        WS[at - LAGS + half : at - LAGS + half + m, 64:128] = x[:m, 64:128]
     inv_i = 1.0 / jnp.sqrt(stat[1:2, :] + 1e-6)
     lags = lag_list[...].reshape(1, LAGS)
     place = lax.broadcasted_iota(I32, (64, LAGS), 0) - MAXLAG
@@ -662,17 +665,20 @@
     c64 = lax.broadcasted_iota(I32, (64, 64), 1)
     sea = mask[...].reshape(1, 64).astype(F32)
     sea = jnp.sum(jnp.where(r64 == c64, sea, 0.0), axis=1, keepdims=True)
-    for k in range(KC):
-        x = WS[LAGS * k : LAGS * k + 64, 0:64]
+    terms = []
+    for k in range(0, KC, 2):
+        x = WS[LAGS * k : LAGS * k + 64, :]
         hi = x.astype(BF)
         x = x - hi.astype(F32)
         mid = x.astype(BF)
         lo = (x - mid.astype(F32)).astype(BF)
-        y = lax.dot_general(
-            jnp.concatenate([hi, mid, lo], axis=0), pick, (((0,), (0,)), ((), ())),
-            preferred_element_type=F32,
-        )
-        out[k] = y * inv_i[:, k : k + 1] * sea
+        terms.append(jnp.concatenate([hi, mid, lo], axis=0))
+    y = lax.dot_general(
+        jnp.concatenate(terms, axis=1), pick, (((0,), (0,)), ((), ())),
+        preferred_element_type=F32,
+    )
+    for k in range(KC):
+        out[k] = y[64 * k : 64 * k + 64] * inv_i[:, k : k + 1] * sea
         pltpu.make_async_copy(out.at[k], out_hbm.at[k], sem.at[k]).start()
     for k in range(KC):
         pltpu.make_async_copy(out.at[k], out_hbm.at[k], sem.at[k]).wait()
@@ -734,9 +740,9 @@
             dma,
             dma,
             dma((6, 4)),
-            dma((3, 2, 4)),
+            dma((3, 4)),
             dma((6,)),
-            dma((3, 2)),
+            dma((3,)),
             dma((3,)),
             dma,
             dma,

time: 46.3 us -> 45.6 us (0.985)
  Pallas kernels: 46.1 us -> 45.4 us
    pallas_call x1, Pallas kernels: 44.6 us -> 44.1 us  [shards(): pl.pallas_call(main_kernel, out_shape=(jax.ShapeDtypeStruct((3, 16 * HG,...]
where the time goes in v2:
time: 45.6 us; the launch traced here: 45.4 us
  Pallas kernels  45.4 us (100%)
    pallas_call x1, Pallas kernels, shards(): pl.pallas_call(main_kernel, out_shape=(jax.ShapeDtypeStruct((3, 16 * HG,...  44.1 us
    pallas_call x1, Pallas kernels, shards(): pl.pallas_call(last_kernel, out_shape=jax.ShapeDtypeStruct((KC, CELLS //...  1.28 us

profile of v2, /device:TPU:1, one launch (start us, length us, event | category | flops | bytes accessed | tf_op | source)
XLA Modules:
  0.0 45.4 jit_solution(8299984244440222785)
XLA Ops:
  0.0 0.0 copy-start.1
  0.0 0.0 copy-start
  0.0 44.1 %shard_map.55 = (f32[3,112,128]{2,1,0:T(8,128)S(1)}, f32[8,128]{1,0:T(8,128)S(1)}, f32[8,128]{1,0:T(8,128)S(1)}, f32[8,128]{1,0:T(8,128)S(1)}) custom-call(bf16[336,8192]{1,0:T(8,128)(2,1)} %field.1, f32[10,336]{1,0:T(8,128)} %bitcast.2, s32[10]{0:T(128)} %offs_in.1), custom_call_target="tpu_custom_call" | custom-call | tf_op jit(solution)/shard_map/pallas_call | solution.py:691
  44.1 0.0 copy-done.1
  44.1 0.0 copy-done
  44.2 1.3 %shard_map.56 = f32[10,64,61]{2,1,0:T(8,128)} custom-call(f32[3,112,128]{2,1,0:T(8,128)S(1)} %get-tuple-element.9.fin, f32[8,128]{1,0:T(8,128)S(1)} %get-tuple-element.10.sums, f32[8,128]{1,0:T(8,128)S(1)} %get-tuple-element.11.tot, f32[8,128]{1,0:T(8,128)S(1)} %get-tuple-element.12.stat, s32[61]{0:T(128)S(1)} %copy-done, s32[64]{0:T(128)S(1)} %copy-done.1), custom_call_target="tpu_custom_call" | custom-call | tf_op jit(solution)/shard_map/pallas_call | solution.py:763
Async XLA Ops:
  0.0 44.1 %copy-start.1 = (s32[64]{0:T(128)S(1)}, s32[64]{0:T(128)}, u32[]{:S(2)}) copy-start(s32[64]{0:T(128)} %mask.1) | copy-start | bytes 772
  0.0 44.1 %copy-start = (s32[61]{0:T(128)S(1)}, s32[61]{0:T(128)}, u32[]{:S(2)}) copy-start(s32[61]{0:T(128)} %lag_list.1) | copy-start | bytes 736

commit v3 on v2

--- a/solution.py
+++ b/solution.py
@@ -106,7 +106,7 @@
 
 
 def main_kernel(
-    field, idx_in, offs_in, fin, sums_o, tot_o, stat_o,
+    field, idx_in, offs_in, fin, sums_o, stat_o,
     idx, offs, sem_in, F, W, WF, OH, acc, NP, S1,
     s_far, r_far, s_n, r_n, s2f, r2f, s2n, r2n, s3, r3,
     iw, ipad, bs, g1, g2, fsum, sx_s, sx_r, tb1, sy_s, sy_r, tb3,
@@ -133,8 +133,9 @@
         return peer(dx=f0 * delta, dy=f1 * delta, dz=f2 * delta, dc=dc)
 
     partner = peer(dc=1)
-    xpeers = [(dx, dc) for dx in range(4) for dc in range(2) if dx or dc]
+    xpeers = [(dx, dc) for dx in (2, 1, 3, 0) for dc in (1, 0) if dx or dc]
     yzpeers = [(dy, dz) for dy in range(4) for dz in range(4) if dy or dz]
+    yzpeers.sort(key=lambda v: -min(v[0], 4 - v[0]) - min(v[1], 4 - v[1]))
     q_next, q_prev = (Q + 1) % N_CHIP, (Q + N_CHIP - 1) % N_CHIP
 
     copies = [
@@ -149,10 +150,10 @@
     def greet(device):
         pl.semaphore_signal(barrier, inc=1, device_id=device, device_id_type=MESH)
 
+    for dy, dz in yzpeers:
+        greet(peer(dy=dy, dz=dz))
     for dx, dc in xpeers:
         greet(peer(dx=dx, dc=dc))
-    for dy, dz in yzpeers:
-        greet(peer(dy=dy, dz=dz))
     for d in range(1, 4):
         greet(peer(dy=d, dc=1))
         greet(peer(dz=d, dc=1))
@@ -178,6 +179,7 @@
     for c in copies:
         c.wait()
     mine = idx[...]
+    final = (C + X + Y + Z) % 2 == 0
     me8, me16 = X * 2 + C, Y * 4 + Z
     g1[me8, 0:1, :] = as_row(jnp.sum(mine, axis=1, keepdims=True))
     g1[me8, 1:2, :] = as_row(jnp.sum(mine * mine, axis=1, keepdims=True))
@@ -412,11 +414,14 @@
             send_n(u, dr, i)
             if i == 0:
                 send_far(u, 3)
-            if 0 < i < 3:
-                send_n(u, 1 - dr, i + 1)
+            if i == 1:
+                send_n(u, 1 - dr, 2)
+            if i == 3:
+                send_n(u, 1 - dr, 3)
 
     near_sum(0)
     near_sum(1)
+    near_sum(2)
 
     @pl.loop(0, 3)
     def _(p):
@@ -474,6 +479,7 @@
         c = remote(to, sx_r.at[d - 1], sem_ss.at[0], sem_sr.at[0], peer(dx=d))
         c.start()
 
+
     @pl.loop(0, 3)
     def _(p):
         arrived(p, 0)
@@ -498,7 +504,6 @@
         add_tile(u, i, lambda g: r2f[u, rows(g), :])
         near2(p, i, dr, dr)
 
-    near_sum(2)
     near_sum(3)
 
     @pl.loop(0, 3)
@@ -509,6 +514,15 @@
     @pl.loop(0, 3)
     def _(p):
         near2_sum(p, 1, C)
+
+    @pl.loop(0, 3)
+    def _(p):
+        arrived(p, 2)
+        near2(p, 2, 1 - C, C)
+
+    @pl.loop(0, 3)
+    def _(p):
+        near2_sum(p, 2, 1 - C)
 
     pltpu.make_async_copy(sx_r, sx_r, sem_sr.at[0]).wait()
     tb1[...] = (tb1[...] + sx_r[0]) + (sx_r[1] + sx_r[2])
@@ -519,27 +533,26 @@
         dst[1:2, :] = tb1[pl.ds(8 + i, 1), :]
         dst[2:8, :] = tb1[16:22, :]
 
-    for n, (dy, dz) in enumerate(yzpeers):
-        side_rows(sy_s.at[n], (Y + dy) % 4, (Z + dz) % 4)
-        c = remote(
-            sy_s.at[n], sy_r.at[n], sem_ss.at[1], sem_sr.at[1], peer(dy=dy, dz=dz)
-        )
-        c.start()
-
-    @pl.loop(0, 3)
-    def _(p):
-        arrived(p, 2)
-        near2(p, 2, 1 - C, C)
-
-    @pl.loop(0, 3)
-    def _(p):
-        near2_sum(p, 2, 1 - C)
+    def side_send(odd):
+        some = [(dy, dz) for dy, dz in yzpeers if (dy + dz) % 2 == odd]
+        for n, (dy, dz) in enumerate(some):
+            side_rows(sy_s.at[n], (Y + dy) % 4, (Z + dz) % 4)
+            remote(
+                sy_s.at[n], sy_r.at[7 * odd + n], sem_ss.at[1], sem_sr.at[1], peer(dy=dy, dz=dz)
+            ).start()
+
+    @pl.when(final)
+    def _():
+        side_send(0)
+
+    @pl.when(jnp.logical_not(final))
+    def _():
+        side_send(1)
 
     @pl.loop(0, 3)
     def _(p):
         arrived(p, 3)
 
-    final = (C + X + Y + Z) % 2 == 0
     lane16 = lax.broadcasted_iota(I32, (16, 128), 1)
 
     @pl.loop(0, 3)
@@ -580,15 +593,13 @@
             for i, delta in enumerate((1, 3)):
                 last_send(2 * p + ((d + delta) % 4) // 2, i, delta)
 
-    side_rows(tb3, Y, Z)
-    total = tb3[...]
-    pltpu.make_async_copy(sy_r, sy_r, sem_sr.at[1]).wait()
-    for n in range(15):
-        total = total + sy_r[n]
-    tot_o[...] = total
-
     @pl.when(final)
     def _():
+        pltpu.make_async_copy(sy_r, sy_r, sem_sr.at[1]).wait()
+        side_rows(tb3, Y, Z)
+        total = tb3[...]
+        for n in range(15):
+            total = total + sy_r[n]
         sums_o[...] = total
         remote(sums_o, sums_o, sem_os, sem_or, partner).start()
 
@@ -609,12 +620,14 @@
     def _():
         pltpu.make_async_copy(bs, bs, sem_bs).wait()
         pltpu.make_async_copy(sums_o, sums_o, sem_os).wait()
+        settle(sy_s, (pl.ds(0, 7),), sem_ss.at[1])
         for h in range(2):
             pltpu.make_async_copy(s3.at[:, 2, h], s3.at[:, 2, h], sem_s3.at[h]).wait()
 
     @pl.when(jnp.logical_not(final))
     def _():
         pltpu.make_async_copy(sums_o, sums_o, sem_or).wait()
+        settle(sy_s, (pl.ds(0, 8),), sem_ss.at[1])
         for h in range(2):
             pltpu.make_async_copy(s3.at[:, 0:2, h], s3.at[:, 0:2, h], sem_s3.at[h]).wait()
 
@@ -622,13 +635,12 @@
     settle(g2, (pl.ds(0, 15),), sem_gs.at[1])
     pltpu.make_async_copy(iw, iw, sem_is).wait()
     pltpu.make_async_copy(sx_s, sx_s, sem_ss.at[0]).wait()
-    pltpu.make_async_copy(sy_s, sy_s, sem_ss.at[1]).wait()
     pltpu.make_async_copy(F.at[:, own_days, :], F.at[:, own_days, :], sem_fs).wait()
     for buf, sem in ((s_far, sem_sfar), (s_n, sem_sn), (s2f, sem_s2f), (s2n, sem_s2n)):
         pltpu.make_async_copy(buf, buf, sem).wait()
 
 
-def last_kernel(fin, sums, tot, stat, lag_list, mask, out_hbm, WS, out, sem):
+def last_kernel(fin, sums, stat, lag_list, mask, out_hbm, WS, out, sem):
     core = lax.axis_index("core")
     n = float(TDAYS)
     half = 16 * HG
@@ -644,7 +656,7 @@
     left = lax.broadcasted_iota(I32, (half, 128), 1) < 64
     WS[KC * LAGS - LAGS - 5 : KC * LAGS + 6, :] = jnp.zeros((LAGS + 11, 128), F32)
     for p in range(3):
-        t = jnp.concatenate([tot[2 * p + 2 : 2 * p + 3, :], tot[2 * p + 3 : 2 * p + 4, :]], axis=1)
+        t = jnp.concatenate([sums[2 * p + 2 : 2 * p + 3, :], sums[2 * p + 3 : 2 * p + 4, :]], axis=1)
         t0 = jnp.sum(jnp.where(row == col, t, 0.0), axis=1, keepdims=True)
         t1 = jnp.sum(jnp.where(row + half == col, t, 0.0), axis=1, keepdims=True)
         x = (fin[p] - mean_x * jnp.where(left, t0, t1)) * inv
@@ -688,16 +700,15 @@
     vmem = pl.BlockSpec(memory_space=pltpu.VMEM)
     i16 = jnp.int16
     dma = pltpu.SemaphoreType.DMA
-    fin, sums, tot, stat = pl.pallas_call(
+    fin, sums, stat = pl.pallas_call(
         main_kernel,
         out_shape=(
             jax.ShapeDtypeStruct((3, 16 * HG, 128), F32),
             jax.ShapeDtypeStruct((8, 128), F32),
             jax.ShapeDtypeStruct((8, 128), F32),
-            jax.ShapeDtypeStruct((8, 128), F32),
         ),
         in_specs=[pl.BlockSpec(memory_space=pltpu.HBM)] * 3,
-        out_specs=(vmem, vmem, vmem, vmem),
+        out_specs=(vmem, vmem, vmem),
         scratch_shapes=[
             pltpu.VMEM((KC, T_DEV), F32),
             pltpu.SMEM((KC,), I32),
@@ -728,7 +739,7 @@
             pltpu.VMEM((3, 24, 128), F32),
             pltpu.VMEM((3, 24, 128), F32),
             pltpu.VMEM((24, 128), F32),
-            pltpu.VMEM((15, 8, 128), F32),
+            pltpu.VMEM((8, 8, 128), F32),
             pltpu.VMEM((15, 8, 128), F32),
             pltpu.VMEM((8, 128), F32),
             dma,
@@ -763,7 +774,7 @@
     maps = pl.pallas_call(
         last_kernel,
         out_shape=jax.ShapeDtypeStruct((KC, CELLS // 128, LAGS), F32),
-        in_specs=[vmem] * 6,
+        in_specs=[vmem] * 5,
         out_specs=pl.BlockSpec(memory_space=pltpu.HBM),
         scratch_shapes=[
             pltpu.VMEM((616, 128), F32),
@@ -771,7 +782,7 @@
             dma((KC,)),
         ],
         compiler_params=pltpu.CompilerParams(vmem_limit_bytes=8 * 1024 * 1024),
-    )(fin, sums, tot, stat, lag_list, sea_mask)
+    )(fin, sums, stat, lag_list, sea_mask)
     return jnp.transpose(maps, (1, 0, 2))
 
 

time: 45.6 us -> 45.4 us (level)
  no operation moved by 1% of the time
where the time goes in v3:
time: 45.4 us; the launch traced here: 45.3 us
  Pallas kernels  45.2 us (100%)
    pallas_call x1, Pallas kernels, shards(): pl.pallas_call(main_kernel, out_shape=(jax.ShapeDtypeStruct((3, 16 * HG,...  43.9 us
    pallas_call x1, Pallas kernels, shards(): pl.pallas_call(last_kernel, out_shape=jax.ShapeDtypeStruct((KC, CELLS //...  1.28 us

profile of v3, /device:TPU:1, one launch (start us, length us, event | category | flops | bytes accessed | tf_op | source)
XLA Modules:
  0.0 45.3 jit_solution(1006065381718460196)
XLA Ops:
  0.0 0.0 copy-start.1
  0.0 0.0 copy-start
  0.0 43.9 %shard_map.55 = (f32[3,112,128]{2,1,0:T(8,128)S(1)}, f32[8,128]{1,0:T(8,128)S(1)}, f32[8,128]{1,0:T(8,128)S(1)}) custom-call(bf16[336,8192]{1,0:T(8,128)(2,1)} %field.1, f32[10,336]{1,0:T(8,128)} %bitcast.2, s32[10]{0:T(128)} %offs_in.1), custom_call_target="tpu_custom_call" | custom-call | tf_op jit(solution)/shard_map/pallas_call | solution.py:703
  44.0 0.0 copy-done.1
  44.0 0.0 copy-done
  44.0 1.3 %shard_map.56 = f32[10,64,61]{2,1,0:T(8,128)} custom-call(f32[3,112,128]{2,1,0:T(8,128)S(1)} %get-tuple-element.8.fin, f32[8,128]{1,0:T(8,128)S(1)} %get-tuple-element.9.sums, f32[8,128]{1,0:T(8,128)S(1)} %get-tuple-element.10.stat, s32[61]{0:T(128)S(1)} %copy-done, s32[64]{0:T(128)S(1)} %copy-done.1), custom_call_target="tpu_custom_call" | custom-call | tf_op jit(solution)/shard_map/pallas_call | solution.py:774
Async XLA Ops:
  0.0 44.0 %copy-start.1 = (s32[64]{0:T(128)S(1)}, s32[64]{0:T(128)}, u32[]{:S(2)}) copy-start(s32[64]{0:T(128)} %mask.1) | copy-start | bytes 772
  0.0 44.0 %copy-start = (s32[61]{0:T(128)S(1)}, s32[61]{0:T(128)}, u32[]{:S(2)}) copy-start(s32[61]{0:T(128)} %lag_list.1) | copy-start | bytes 736

commit v4 on v3

--- a/solution.py
+++ b/solution.py
@@ -313,14 +313,19 @@
     mean_row = g[0:1, :] / float(TDAYS)
     stat_o[...] = jnp.zeros((8, 128), F32)
     stat_o[0:1, :] = mean_row
-    stat_o[1:2, :] = g[1:2, :] / float(TDAYS) - mean_row * mean_row
+    var_row = g[1:2, :] / float(TDAYS) - mean_row * mean_row
+    stat_o[1:2, :] = var_row
+    size_row = jnp.exp2(-jnp.ceil(0.5 * jnp.log2(jnp.maximum(var_row, 0.0) + 1e-6)))
+    stat_o[2:3, :] = size_row
 
     def center(p):
         col = jnp.sum(OH[p] * mean_row, axis=1, keepdims=True)
+        size = jnp.sum(OH[p] * size_row, axis=1, keepdims=True)
         for g in range(G):
             x = WF[p, rows(g), :]
-            x = jnp.where(x > 0.5 * FAR, 0.0, x - col[16 * g : 16 * g + 16])
-            W[p, rows(g), :] = x.astype(BF)
+            y = (x - col[16 * g : 16 * g + 16]).astype(BF).astype(F32)
+            y = y * size[16 * g : 16 * g + 16]
+            W[p, rows(g), :] = jnp.where(x > 0.5 * FAR, 0.0, y).astype(BF)
 
     pltpu.make_async_copy(F.at[:, own_days, :], F.at[:, own_days, :], sem_fr).wait()
 
@@ -668,7 +673,7 @@
         cut = max(0, LAGS - at)
         WS[at - LAGS + cut : at - LAGS + half, 64:128] = y[cut:, 64:128]
         WS[at - LAGS + half : at - LAGS + half + m, 64:128] = x[:m, 64:128]
-    inv_i = 1.0 / jnp.sqrt(stat[1:2, :] + 1e-6)
+    inv_i = 1.0 / (jnp.sqrt(stat[1:2, :] + 1e-6) * stat[2:3, :])
     lags = lag_list[...].reshape(1, LAGS)
     place = lax.broadcasted_iota(I32, (64, LAGS), 0) - MAXLAG
     pick = (place == lags).astype(F32).astype(BF)

time: 45.4 us -> 45.5 us (level)
  no operation moved by 1% of the time
where the time goes in v4:
time: 45.5 us; the launch traced here: 45.3 us
  Pallas kernels  45.3 us (100%)
    pallas_call x1, Pallas kernels, shards(): pl.pallas_call(main_kernel, out_shape=(jax.ShapeDtypeStruct((3, 16 * HG,...  44 us
    pallas_call x1, Pallas kernels, shards(): pl.pallas_call(last_kernel, out_shape=jax.ShapeDtypeStruct((KC, CELLS //...  1.28 us

profile of v4, /device:TPU:1, one launch (start us, length us, event | category | flops | bytes accessed | tf_op | source)
XLA Modules:
  0.0 45.3 jit_solution(2208095881958053778)
XLA Ops:
  0.0 0.0 copy-start.1
  0.0 0.0 copy-start
  0.0 44.0 %shard_map.55 = (f32[3,112,128]{2,1,0:T(8,128)S(1)}, f32[8,128]{1,0:T(8,128)S(1)}, f32[8,128]{1,0:T(8,128)S(1)}) custom-call(bf16[336,8192]{1,0:T(8,128)(2,1)} %field.1, f32[10,336]{1,0:T(8,128)} %bitcast.2, s32[10]{0:T(128)} %offs_in.1), custom_call_target="tpu_custom_call" | custom-call | tf_op jit(solution)/shard_map/pallas_call | solution.py:708
  44.0 0.0 copy-done.1
  44.0 0.0 copy-done
  44.0 1.3 %shard_map.56 = f32[10,64,61]{2,1,0:T(8,128)} custom-call(f32[3,112,128]{2,1,0:T(8,128)S(1)} %get-tuple-element.8.fin, f32[8,128]{1,0:T(8,128)S(1)} %get-tuple-element.9.sums, f32[8,128]{1,0:T(8,128)S(1)} %get-tuple-element.10.stat, s32[61]{0:T(128)S(1)} %copy-done, s32[64]{0:T(128)S(1)} %copy-done.1), custom_call_target="tpu_custom_call" | custom-call | tf_op jit(solution)/shard_map/pallas_call | solution.py:779
Async XLA Ops:
  0.0 44.0 %copy-start.1 = (s32[64]{0:T(128)S(1)}, s32[64]{0:T(128)}, u32[]{:S(2)}) copy-start(s32[64]{0:T(128)} %mask.1) | copy-start | bytes 772
  0.0 44.0 %copy-start = (s32[61]{0:T(128)S(1)}, s32[61]{0:T(128)}, u32[]{:S(2)}) copy-start(s32[61]{0:T(128)} %lag_list.1) | copy-start | bytes 736
